TPU v7x, 128 devices: a whole 4x4x4 slice. The times are simulated.
128 devices in a mesh: data: 1, time: 128 (over z, y, x, core).
Axes of the slice: x: 4, y: 4, z: 4, core: 2. Of those that a mesh axis runs over, the one named last changes fastest.
Arguments:
- x_init: float32 [1, 4096, 64], P('data')
- w_in: bfloat16 [64, 1536], replicated
- w_out: bfloat16 [1536, 64], replicated
- mod_scale: bfloat16 [128, 1536], P('time')
- mod_shift: bfloat16 [128, 1536], P('time')
- step_size: float32 [128], P('time')
Outputs:
- output: float32 [128, 1, 4096, 64], P('time', 'data')
All inputs are finite; a program needn't handle non-finite values.
Results may differ from a plain program's by a relative error of at most 0.001.
Values are sent between devices in bfloat16 or wider.
A program may use at most 1 GiB of HBM per device.

v0:
```python
import functools

import jax
import jax.numpy as jnp
from jax import lax
from jax.experimental import pallas as pl
from jax.experimental.pallas import tpu as pltpu
from jax.sharding import PartitionSpec as P

SWEEPS = 4
C0 = 0.7978845608028654
C1 = C0 * 0.044715
STEPS_PER_BLOCK = 16
TILE = 256


def half_gelu(h):
    t = jnp.tanh(h * (h * h * (8.0 * C1) + 2.0 * C0))
    return h + h * t


def kernel(n_time, tok, x_hbm, w1_ref, w2t_ref, scale_ref, shift_ref, step_ref, out_ref,
           xcol, xrow, w2, mod_send, mod_recv, mods, p0, xbf, send, prefix,
           x_sem, mod_send_sem, mod_recv_sem, out_send_sem, out_recv_sem):
    me = lax.axis_index('time')
    hidden = w1_ref.shape[1]
    chans = w1_ref.shape[0]
    n_rows = hidden // 128
    per_col = 128 // tok

    x_copy = pltpu.make_async_copy(
        x_hbm.at[:, pl.ds(pl.multiple_of((me // per_col) * 128, 128), 128)], xcol, x_sem)
    x_copy.start()

    for c in range(n_rows):
        mod_send[pl.ds(c, 1), :] = scale_ref[:, c * 128:(c + 1) * 128]
        mod_send[pl.ds(n_rows + c, 1), :] = shift_ref[:, c * 128:(c + 1) * 128]
    step = jnp.broadcast_to(step_ref[...], (1, 128))
    high = step.astype(jnp.bfloat16)
    rest = step - high.astype(jnp.float32)
    mid = rest.astype(jnp.bfloat16)
    low = (rest - mid.astype(jnp.float32)).astype(jnp.bfloat16)
    mod_send[pl.ds(2 * n_rows, 1), :] = high
    mod_send[pl.ds(2 * n_rows + 1, 1), :] = mid
    mod_send[pl.ds(2 * n_rows + 2, 1), :] = low

    def send_mod(k, carry):
        dst = lax.rem(me + k, n_time)
        pltpu.make_async_remote_copy(
            src_ref=mod_send, dst_ref=mod_recv.at[me], send_sem=mod_send_sem, recv_sem=mod_recv_sem,
            device_id={'time': dst}, device_id_type=pl.DeviceIdType.MESH).start()
        return carry

    lax.fori_loop(1, n_time, send_mod, 0)
    mod_recv[me] = mod_send[...]

    w2[...] = w2t_ref[...].astype(jnp.float32).T.astype(jnp.bfloat16)
    x_copy.wait()
    xrow[...] = xcol[...].T
    x0 = xrow[pl.ds(pl.multiple_of(lax.rem(me, per_col) * tok, tok), tok), :]
    for n in range(hidden // TILE):
        p0[:, n * TILE:(n + 1) * TILE] = jnp.dot(
            x0.astype(jnp.bfloat16), w1_ref[:, n * TILE:(n + 1) * TILE], preferred_element_type=jnp.float32)

    pltpu.make_async_copy(mod_recv.at[pl.ds(0, n_time - 1)], mod_recv.at[pl.ds(0, n_time - 1)], mod_recv_sem).wait()
    pltpu.make_async_copy(mod_recv.at[pl.ds(0, n_time - 1)], mod_recv.at[pl.ds(0, n_time - 1)], mod_send_sem).wait()

    def unpack(j, carry):
        block = mod_recv[j].astype(jnp.float32)
        mods[j, pl.ds(0, n_rows), :] = 0.5 * (1.0 + block[:n_rows])
        mods[j, pl.ds(n_rows, n_rows), :] = 0.5 * block[n_rows:2 * n_rows]
        mods[j, pl.ds(2 * n_rows, 1), :] = (block[2 * n_rows:2 * n_rows + 1] + block[2 * n_rows + 1:2 * n_rows + 2]) + block[2 * n_rows + 2:2 * n_rows + 3]
        return carry

    lax.fori_loop(0, n_time, unpack, 0, unroll=4)

    rows = STEPS_PER_BLOCK * tok

    def block_step(sweep, b, carry):
        acc = None
        if sweep > 0:
            x = xbf[pl.ds(pl.multiple_of(b * rows, rows), rows), :]
        for n in range(hidden // TILE):
            if sweep > 0:
                pre = jnp.dot(x, w1_ref[:, n * TILE:(n + 1) * TILE], preferred_element_type=jnp.float32)
            parts = []
            for s in range(STEPS_PER_BLOCK):
                j = b * STEPS_PER_BLOCK + s
                halves = []
                for half in range(TILE // 128):
                    c = n * (TILE // 128) + half
                    gain = mods[j, pl.ds(c, 1), :]
                    shift = mods[j, pl.ds(n_rows + c, 1), :]
                    if sweep > 0:
                        p = pre[s * tok:(s + 1) * tok, half * 128:(half + 1) * 128]
                    else:
                        p = p0[:, c * 128:(c + 1) * 128]
                    halves.append(half_gelu(p * gain + shift).astype(jnp.bfloat16))
                parts.append(jnp.concatenate(halves, axis=1))
            act = jnp.concatenate(parts, axis=0)
            prod = jnp.dot(act, w2[n * TILE:(n + 1) * TILE, :], preferred_element_type=jnp.float32)
            acc = prod if acc is None else acc + prod
        total = prefix[...]
        for s in range(STEPS_PER_BLOCK):
            j = b * STEPS_PER_BLOCK + s
            new = x0 + total
            if sweep < SWEEPS - 1:
                xbf[pl.ds(pl.multiple_of(j * tok, tok), tok), :] = new.astype(jnp.bfloat16)
            else:
                send[j, :, 0:chans] = new[:tok // 2]
                send[j, :, chans:2 * chans] = new[tok // 2:]
            total = total + mods[j, pl.ds(2 * n_rows, 1), :][:, :chans] * acc[s * tok:(s + 1) * tok, :]
        prefix[...] = total
        return carry

    for sweep in range(SWEEPS):
        prefix[...] = jnp.zeros_like(prefix)
        lax.fori_loop(0, n_time // STEPS_PER_BLOCK, functools.partial(block_step, sweep), 0)

    def send_out(k, carry):
        dst = lax.rem(me + k, n_time)
        pltpu.make_async_remote_copy(
            src_ref=send.at[dst], dst_ref=out_ref.at[me], send_sem=out_send_sem, recv_sem=out_recv_sem,
            device_id={'time': dst}, device_id_type=pl.DeviceIdType.MESH).start()
        return carry

    lax.fori_loop(1, n_time, send_out, 0)
    out_ref[me] = send[me]
    pltpu.make_async_copy(send.at[pl.ds(0, n_time - 1)], send.at[pl.ds(0, n_time - 1)], out_send_sem).wait()
    pltpu.make_async_copy(out_ref.at[pl.ds(0, n_time - 1)], out_ref.at[pl.ds(0, n_time - 1)], out_recv_sem).wait()


def solution(mesh):
    n_time = mesh.shape['time']

    def per_device(x_init, w_in, w_out, mod_scale, mod_shift, step_size):
        _, tokens, chans = x_init.shape
        hidden = w_in.shape[1]
        tok = tokens // n_time
        vmem = pl.BlockSpec(memory_space=pltpu.VMEM)
        out = pl.pallas_call(
            functools.partial(kernel, n_time, tok),
            out_shape=jax.ShapeDtypeStruct((n_time, tok // 2, 2 * chans), jnp.float32),
            in_specs=[pl.BlockSpec(memory_space=pl.ANY), vmem, vmem, vmem, vmem, vmem],
            out_specs=vmem,
            scratch_shapes=[
                pltpu.VMEM((chans, 128), jnp.float32),
                pltpu.VMEM((128, chans), jnp.float32),
                pltpu.VMEM((hidden, chans), jnp.bfloat16),
                pltpu.VMEM((32, 128), jnp.bfloat16),
                pltpu.VMEM((n_time, 32, 128), jnp.bfloat16),
                pltpu.VMEM((n_time, 32, 128), jnp.float32),
                pltpu.VMEM((tok, hidden), jnp.float32),
                pltpu.VMEM((n_time * tok, chans), jnp.bfloat16),
                pltpu.VMEM((n_time, tok // 2, 2 * chans), jnp.float32),
                pltpu.VMEM((tok, chans), jnp.float32),
            ] + [pltpu.SemaphoreType.DMA] * 5,
            compiler_params=pltpu.CompilerParams(has_side_effects=True),
            name='sweeps',
        )(x_init[0].T, w_in, w_out.T, mod_scale, mod_shift, step_size[None])
        out = out.reshape(n_time, tok // 2, 2, chans).transpose(0, 2, 1, 3)
        return out.reshape(1, 1, tokens, chans)

    return jax.shard_map(per_device, mesh=mesh, in_specs=(P('data'), P(), P(), P('time'), P('time'), P('time')), out_specs=P('time', 'data'), check_vma=False)
```

profile of v0, /device:TPU:1, one launch (start us, length us, event | category | flops | bytes accessed | tf_op | source)
XLA Modules:
  0.0 94.7 jit_solution(14143176664054861628)
XLA Ops:
  0.7 89.0 %sweeps.1 = f32[128,16,128]{2,1,0:T(8,128)} custom-call(f32[64,4096]{1,0:T(8,128)} %bitcast.12, bf16[64,1536]{1,0:T(8,128)(2,1)} %w1_ref.1, bf16[64,1536]{1,0:T(8,128)(2,1)} %bitcast.13, bf16[1,1536]{1,0:T(2,128)(2,1)} %scale_ref.1, bf16[1,1536]{1,0:T(2,128)(2,1)} %shift_ref.1, f32[1,1]{1,0:T(1,128)} %bitcast.9.step_ref), custom_call_target="tpu_custom_call" | custom-call | tf_op jit(solution)/shard_map/sweeps/pallas_call | solution.py:141
  89.7 1.6 %copy.8 = f32[128,16,128]{0,2,1:T(8,128)S(1)} copy(f32[128,16,128]{2,1,0:T(8,128)} %sweeps.1) | data formatting | bytes 2097152 | tf_op jit(solution)/shard_map/sweeps/pallas_call | solution.py:141
  91.3 1.8 %copy.9 = f32[128,2,16,64]{3,2,1,0:T(8,128)S(1)} copy(f32[128,2,16,64]{0,3,1,2:T(8,128)S(1)} %bitcast.11) | data formatting | bytes 2097152 | tf_op jit(solution)/shard_map/transpose | solution.py:161
  93.1 1.6 %copy.10 = f32[1,1,4096,64]{2,3,1,0:T(8,128)} copy(f32[1,1,4096,64]{3,2,1,0:T(8,128)S(1)} %bitcast.10) | data formatting | bytes 2097152 | tf_op jit(solution)/shard_map/reshape | solution.py:162
where the time goes:
time: 94.8 us; the launch traced here: 94.7 us
  Pallas kernels  89 us (94%)
  local copies, waits for them, and re-layouts  4.98 us (5%)
    pallas_call x1, Pallas kernels, per_device(): pl.pallas_call(functools.partial(kernel, n_time, tok), out_shape=jax.Shap...  89 us

commit v1 on v0

v1 whole, which is shorter than its diff:
```python
import functools

import jax
import jax.numpy as jnp
from jax import lax
from jax.experimental import pallas as pl
from jax.experimental.pallas import tpu as pltpu
from jax.sharding import PartitionSpec as P

SWEEPS = 4
C0 = 0.7978845608028654
C1 = C0 * 0.044715
TILE = 256
ROWS = 512
CHUNKS = 2
GROUP = 8
CHIP_STRIDE = 27
DEV_STRIDE = 45
MESH = pl.DeviceIdType.MESH


def half_gelu(h):
    t = jnp.tanh(h * (h * h * (8.0 * C1) + 2.0 * C0))
    return h + h * t


def wait_bytes(ref, sem):
    pltpu.make_async_copy(ref, ref, sem).wait()


def kernel(n_time, x_hbm, w1_ref, w2t_ref, scale_ref, shift_ref, step_ref, out_ref,
           xcol, xrow, w2, mod_send, mod_recv, mods, p0, xbf, send, prefix,
           x_sem, mod_send_sem, mod_recv_sem, pair_send_sem, pair_recv_sem, out_send_sem, out_recv_sem):
    me = lax.axis_index('time')
    n_chips = n_time // 2
    chip = me // 2
    core = lax.rem(me, 2)
    partner = me + 1 - 2 * core
    chans, hidden = w1_ref.shape
    n_rows = hidden // 128
    tok = 2 * GROUP
    tokens = x_hbm.shape[1]

    barrier = pltpu.get_barrier_semaphore()

    def arrive(k, carry):
        pl.semaphore_signal(barrier, inc=1, device_id={'time': lax.rem(me + k * DEV_STRIDE, n_time)}, device_id_type=MESH)
        return carry

    lax.fori_loop(1, n_time, arrive, 0)

    x_copies = []
    for q in range(CHUNKS):
        for half in range(2):
            start = half * (tokens // 2) + q * (tokens // 2 // CHUNKS) + (me * GROUP // 128) * 128
            x_copies.append(pltpu.make_async_copy(
                x_hbm.at[:, pl.ds(pl.multiple_of(start, 128), 128)], xcol.at[2 * q + half], x_sem.at[2 * q + half]))
            x_copies[-1].start()

    for c in range(n_rows):
        mod_send[pl.ds(c, 1), :] = scale_ref[:, c * 128:(c + 1) * 128]
        mod_send[pl.ds(n_rows + c, 1), :] = shift_ref[:, c * 128:(c + 1) * 128]
    step = jnp.broadcast_to(step_ref[...], (1, 128))
    high = step.astype(jnp.bfloat16)
    rest = step - high.astype(jnp.float32)
    mid = rest.astype(jnp.bfloat16)
    low = (rest - mid.astype(jnp.float32)).astype(jnp.bfloat16)
    mod_send[pl.ds(2 * n_rows, 1), :] = high
    mod_send[pl.ds(2 * n_rows + 1, 1), :] = mid
    mod_send[pl.ds(2 * n_rows + 2, 1), :] = low

    w2[...] = w2t_ref[...].astype(jnp.float32).T.astype(jnp.bfloat16)
    for copy in x_copies:
        copy.wait()
    for i in range(2 * CHUNKS):
        xrow[i] = xcol[i].T

    def x_tokens(q):
        lo = pl.ds(pl.multiple_of(lax.rem(me * GROUP, 128), GROUP), GROUP)
        return jnp.concatenate([xrow[2 * q, lo, :], xrow[2 * q + 1, lo, :]], axis=0)

    for q in range(CHUNKS):
        x0 = x_tokens(q).astype(jnp.bfloat16)
        for n in range(hidden // TILE):
            p0[q, :, n * TILE:(n + 1) * TILE] = jnp.dot(
                x0, w1_ref[:, n * TILE:(n + 1) * TILE], preferred_element_type=jnp.float32)

    pl.semaphore_wait(barrier, n_time - 1)

    def mod_copy(offset):
        return pltpu.make_async_remote_copy(
            src_ref=mod_send, dst_ref=mod_recv.at[me], send_sem=mod_send_sem, recv_sem=mod_recv_sem.at[offset],
            device_id={'time': lax.rem(chip + offset, n_chips) * 2 + core}, device_id_type=MESH)

    def pair_copy(src, src_ref):
        return pltpu.make_async_remote_copy(
            src_ref=src_ref, dst_ref=mod_recv.at[src], send_sem=pair_send_sem, recv_sem=pair_recv_sem,
            device_id={'time': partner}, device_id_type=MESH)

    def send_mod(k, carry):
        mod_copy(lax.rem(k * CHIP_STRIDE, n_chips)).start()
        return carry

    pair_copy(me, mod_send).start()
    lax.fori_loop(1, n_chips, send_mod, 0)
    mod_recv[me] = mod_send[...]

    def relay(k, carry):
        offset = lax.rem(k * CHIP_STRIDE, n_chips)
        mod_copy(offset).wait_recv()
        src = lax.rem(chip - offset + n_chips, n_chips) * 2 + core
        pair_copy(src, mod_recv.at[src]).start()
        return carry

    lax.fori_loop(1, n_chips, relay, 0)
    half_block = mod_recv.at[pl.ds(0, n_chips)]
    wait_bytes(half_block, pair_recv_sem)
    wait_bytes(half_block, pair_send_sem)
    wait_bytes(mod_recv.at[pl.ds(0, n_chips - 1)], mod_send_sem)

    def unpack(j, carry):
        block = mod_recv[j].astype(jnp.float32)
        mods[j, pl.ds(0, n_rows), :] = 0.5 * (1.0 + block[:n_rows])
        mods[j, pl.ds(n_rows, n_rows), :] = 0.5 * block[n_rows:2 * n_rows]
        mods[j, pl.ds(2 * n_rows, 1), :] = (block[2 * n_rows:2 * n_rows + 1] + block[2 * n_rows + 1:2 * n_rows + 2]) + block[2 * n_rows + 2:2 * n_rows + 3]
        return carry

    lax.fori_loop(0, n_time, unpack, 0, unroll=4)

    steps = ROWS // tok

    def block_step(q, first, b, carry):
        acc = None
        if not first:
            x = xbf[pl.ds(pl.multiple_of(b * ROWS, ROWS), ROWS), :]
        for n in range(hidden // TILE):
            if not first:
                pre = jnp.dot(x, w1_ref[:, n * TILE:(n + 1) * TILE], preferred_element_type=jnp.float32)
            parts = []
            for s in range(steps):
                j = b * steps + s
                halves = []
                for half in range(TILE // 128):
                    c = n * (TILE // 128) + half
                    gain = mods[j, pl.ds(c, 1), :]
                    shift = mods[j, pl.ds(n_rows + c, 1), :]
                    if not first:
                        p = pre[s * tok:(s + 1) * tok, half * 128:(half + 1) * 128]
                    else:
                        p = p0[q, :, c * 128:(c + 1) * 128]
                    halves.append(half_gelu(p * gain + shift).astype(jnp.bfloat16))
                parts.append(jnp.concatenate(halves, axis=1))
            act = jnp.concatenate(parts, axis=0)
            prod = jnp.dot(act, w2[n * TILE:(n + 1) * TILE, :], preferred_element_type=jnp.float32)
            acc = prod if acc is None else acc + prod
        x0 = x_tokens(q)
        total = prefix[...]
        for s in range(steps):
            j = b * steps + s
            new = x0 + total
            xbf[pl.ds(pl.multiple_of(j * tok, tok), tok), :] = new.astype(jnp.bfloat16)
            send[q, j, :, 0:chans] = new[:GROUP]
            send[q, j, :, chans:2 * chans] = new[GROUP:]
            total = total + mods[j, pl.ds(2 * n_rows, 1), :][:, :chans] * acc[s * tok:(s + 1) * tok, :]
        prefix[...] = total
        return carry

    def chunk(q, carry):
        def sweep(first):
            prefix[...] = jnp.zeros_like(prefix)
            lax.fori_loop(0, n_time // steps, functools.partial(block_step, q, first), 0)

        def later_sweep(i, carry):
            sweep(False)
            return carry

        sweep(True)
        lax.fori_loop(1, SWEEPS, later_sweep, 0)

        def send_out(k, carry):
            dst = lax.rem(me + k * DEV_STRIDE, n_time)
            pltpu.make_async_remote_copy(
                src_ref=send.at[q, dst], dst_ref=out_ref.at[q, me], send_sem=out_send_sem, recv_sem=out_recv_sem,
                device_id={'time': dst}, device_id_type=MESH).start()
            return carry

        lax.fori_loop(1, n_time, send_out, 0)
        out_ref[q, me] = send[q, me]
        return carry

    lax.fori_loop(0, CHUNKS, chunk, 0)
    others = out_ref.at[:, pl.ds(0, n_time - 1)]
    wait_bytes(others, out_send_sem)
    wait_bytes(others, out_recv_sem)


def spread(rows_ref, out_ref):
    chans, tokens = out_ref.shape
    for i in range(rows_ref.shape[0] // 128):
        cols = rows_ref[i * 128:(i + 1) * 128, :].T
        out_ref[:, i * 128:(i + 1) * 128] = cols[:chans]
        out_ref[:, tokens // 2 + i * 128:tokens // 2 + (i + 1) * 128] = cols[chans:]


def solution(mesh):
    n_time = mesh.shape['time']

    def per_device(x_init, w_in, w_out, mod_scale, mod_shift, step_size):
        _, tokens, chans = x_init.shape
        hidden = w_in.shape[1]
        tok = 2 * GROUP
        vmem = pl.BlockSpec(memory_space=pltpu.VMEM)
        out = pl.pallas_call(
            functools.partial(kernel, n_time),
            out_shape=jax.ShapeDtypeStruct((CHUNKS, n_time, GROUP, 2 * chans), jnp.float32),
            in_specs=[pl.BlockSpec(memory_space=pl.ANY), vmem, vmem, vmem, vmem, vmem],
            out_specs=vmem,
            scratch_shapes=[
                pltpu.VMEM((2 * CHUNKS, chans, 128), jnp.float32),
                pltpu.VMEM((2 * CHUNKS, 128, chans), jnp.float32),
                pltpu.VMEM((hidden, chans), jnp.bfloat16),
                pltpu.VMEM((32, 128), jnp.bfloat16),
                pltpu.VMEM((n_time, 32, 128), jnp.bfloat16),
                pltpu.VMEM((n_time, 32, 128), jnp.float32),
                pltpu.VMEM((CHUNKS, tok, hidden), jnp.float32),
                pltpu.VMEM((n_time * tok, chans), jnp.bfloat16),
                pltpu.VMEM((CHUNKS, n_time, GROUP, 2 * chans), jnp.float32),
                pltpu.VMEM((tok, chans), jnp.float32),
                pltpu.SemaphoreType.DMA((2 * CHUNKS,)),
                pltpu.SemaphoreType.DMA,
                pltpu.SemaphoreType.DMA((n_time // 2,)),
            ] + [pltpu.SemaphoreType.DMA] * 4,
            compiler_params=pltpu.CompilerParams(has_side_effects=True, collective_id=0),
            name='sweeps',
        )(x_init[0].T, w_in, w_out.T, mod_scale, mod_shift, step_size[None])
        out = pl.pallas_call(
            spread, out_shape=jax.ShapeDtypeStruct((chans, tokens), jnp.float32),
            in_specs=[vmem], out_specs=vmem, name='spread',
        )(out.reshape(tokens // 2, 2 * chans))
        return out.T.reshape(1, 1, tokens, chans)

    return jax.shard_map(per_device, mesh=mesh, in_specs=(P('data'), P(), P(), P('time'), P('time'), P('time')), out_specs=P('time', 'data'), check_vma=False)
```

time: 94.8 us -> 82.5 us (0.87)
  Pallas kernels: 89 us -> 81.6 us
  local copies, waits for them, and re-layouts: 4.98 us -> 0 us
    pallas_call x1 -> x2, Pallas kernels: 89 us -> 81.6 us  [the longest x1 79.1 us: per_device(): pl.pallas_call(functools.partial(kernel, n_time), out_shape=jax.ShapeDtyp...]
    transpose x1 -> x0, local copies, waits for them, and re-layouts: 1.83 us -> none  [per_device(): out = out.reshape(n_time, tok // 2, 2, chans).transpose(0, 2, 1, 3)]
    pallas_call x1 -> x0, local copies, waits for them, and re-layouts: 1.58 us -> none  [per_device(): pl.pallas_call(functools.partial(kernel, n_time, tok), out_shape=jax.Shap...]
    reshape x1 -> x0, local copies, waits for them, and re-layouts: 1.57 us -> none  [per_device(): return out.reshape(1, 1, tokens, chans)]
where the time goes in v1:
time: 82.5 us; the launch traced here: 82.3 us
  Pallas kernels  81.6 us (99%)
    pallas_call x1, Pallas kernels, per_device(): pl.pallas_call(functools.partial(kernel, n_time), out_shape=jax.ShapeDtyp...  79.1 us
    pallas_call x1, Pallas kernels, per_device(): pl.pallas_call(spread, out_shape=jax.ShapeDtypeStruct((chans, tokens), jn...  2.53 us

profile of v1, /device:TPU:1, one launch (start us, length us, event | category | flops | bytes accessed | tf_op | source)
XLA Modules:
  0.0 82.3 jit_solution(15293215184752563031)
XLA Ops:
  0.7 79.1 %sweeps.1 = f32[2,128,8,128]{3,2,1,0:T(8,128)} custom-call(f32[64,4096]{1,0:T(8,128)} %bitcast.11, bf16[64,1536]{1,0:T(8,128)(2,1)} %w1_ref.1, bf16[64,1536]{1,0:T(8,128)(2,1)} %bitcast.12, bf16[1,1536]{1,0:T(2,128)(2,1)} %scale_ref.1, bf16[1,1536]{1,0:T(2,128)(2,1)} %shift_ref.1, f32[1,1]{1,0:T(1,128)} %bitcast.9.step_ref), custom_call_target="tpu_custom_call" | custom-call | tf_op jit(solution)/shard_map/sweeps/pallas_call | solution.py:213
  79.7 2.5 %spread.1 = f32[64,4096]{1,0:T(8,128)} custom-call(f32[2048,128]{1,0:T(8,128)} %bitcast.10), custom_call_target="tpu_custom_call" | custom-call | tf_op jit(solution)/shard_map/spread/pallas_call | solution.py:236

commit v2 on v1

v2 whole, which is shorter than its diff:
```python
import functools

import jax
import jax.numpy as jnp
from jax import lax
from jax.experimental import pallas as pl
from jax.experimental.pallas import tpu as pltpu
from jax.sharding import PartitionSpec as P

SWEEPS = 4
C0 = 0.7978845608028654
C1 = C0 * 0.044715
TILE = 256
ROWS = 1024
CHUNKS = 2
GROUP = 8
SIDE = 4
ARRIVE = 8
DEV_STRIDE = 45
MESH = pl.DeviceIdType.MESH


def half_gelu(h):
    t = jnp.tanh(h * (h * h * (8.0 * C1) + 2.0 * C0))
    return h + h * t


def wait_bytes(ref, sem):
    pltpu.make_async_copy(ref, ref, sem).wait()


def hop(t):
    return t + (t // 2) * (1 - 2 * lax.rem(t, 2))


def chip_at(chip, k, sign):
    pos, out, scale = chip, 0, 1
    for _ in range(3):
        out = out + scale * lax.rem(lax.rem(pos, SIDE) + sign * hop(lax.rem(k, SIDE)) + SIDE, SIDE)
        pos, k, scale = pos // SIDE, k // SIDE, scale * SIDE
    return out


def kernel(n_time, x_hbm, w1_ref, w2t_ref, scale_ref, shift_ref, step_ref, out_ref,
           xcol, xrow, x0, w2, mod_send, mod_recv, mods, p0, drift, xbf, send, recv, prefix,
           x_sem, mod_send_sem, mod_recv_sem, pair_send_sem, pair_recv_sem, out_send_sem, out_recv_sem):
    me = lax.axis_index('time')
    n_chips = n_time // 2
    chip = me // 2
    core = lax.rem(me, 2)
    partner = me + 1 - 2 * core
    chans, hidden = w1_ref.shape
    n_rows = hidden // 128
    tok = 2 * GROUP
    tokens = x_hbm.shape[1]

    barrier = pltpu.get_barrier_semaphore()

    def arrive(k, carry):
        pl.semaphore_signal(barrier, inc=1, device_id={'time': lax.rem(me + k * DEV_STRIDE, n_time)}, device_id_type=MESH)
        return carry

    lax.fori_loop(1, n_time, arrive, 0)

    x_copies = []
    for i in range(2 * CHUNKS):
        start = (i % 2) * (tokens // 2) + (i // 2) * (tokens // 2 // CHUNKS) + (me * GROUP // 128) * 128
        x_copies.append(pltpu.make_async_copy(
            x_hbm.at[:, pl.ds(pl.multiple_of(start, 128), 128)], xcol.at[i], x_sem.at[i]))
        x_copies[-1].start()

    for c in range(n_rows):
        mod_send[pl.ds(c, 1), :] = scale_ref[:, c * 128:(c + 1) * 128]
        mod_send[pl.ds(n_rows + c, 1), :] = shift_ref[:, c * 128:(c + 1) * 128]
    step = jnp.broadcast_to(step_ref[...], (1, 128))
    high = step.astype(jnp.bfloat16)
    rest = step - high.astype(jnp.float32)
    mid = rest.astype(jnp.bfloat16)
    low = (rest - mid.astype(jnp.float32)).astype(jnp.bfloat16)
    mod_send[pl.ds(2 * n_rows, 1), :] = high
    mod_send[pl.ds(2 * n_rows + 1, 1), :] = mid
    mod_send[pl.ds(2 * n_rows + 2, 1), :] = low
    mod_recv[me] = mod_send[...]

    w2[...] = w2t_ref[...].astype(jnp.float32).T.astype(jnp.bfloat16)
    lo = pl.ds(pl.multiple_of(lax.rem(me * GROUP, 128), GROUP), GROUP)
    for i in range(2 * CHUNKS):
        x_copies[i].wait()
        xrow[i] = xcol[i].T
        x0[i * GROUP:(i + 1) * GROUP, :] = xrow[i, lo, :]
    x0_rounded = x0[...].astype(jnp.bfloat16)
    for n in range(hidden // TILE):
        p0[:, n * TILE:(n + 1) * TILE] = jnp.dot(
            x0_rounded, w1_ref[:, n * TILE:(n + 1) * TILE], preferred_element_type=jnp.float32)

    pl.semaphore_wait(barrier, n_time - 1)

    def mod_copy(k):
        return pltpu.make_async_remote_copy(
            src_ref=mod_send, dst_ref=mod_recv.at[me], send_sem=mod_send_sem, recv_sem=mod_recv_sem.at[k],
            device_id={'time': chip_at(chip, k, 1) * 2 + core}, device_id_type=MESH)

    def pair_copy(k, src, src_ref):
        return pltpu.make_async_remote_copy(
            src_ref=src_ref, dst_ref=mod_recv.at[src], send_sem=pair_send_sem, recv_sem=pair_recv_sem.at[k],
            device_id={'time': partner}, device_id_type=MESH)

    def send_mod(k, carry):
        mod_copy(k).start()
        return carry

    def relay(k, carry):
        mod_copy(k).wait_recv()
        src = chip_at(chip, k, -1) * 2 + core
        pair_copy(k, src, mod_recv.at[src]).start()
        return carry

    def pair_wait(k, carry):
        pair_copy(k, me, mod_send).wait_recv()
        return carry

    pair_copy(0, me, mod_send).start()
    lax.fori_loop(1, n_chips, send_mod, 0)
    lax.fori_loop(1, ARRIVE, relay, 0)

    def first_sweep(g, carry):
        lax.fori_loop((g + 1) * ARRIVE, jnp.minimum((g + 2) * ARRIVE, n_chips), relay, 0)
        lax.fori_loop(g * ARRIVE, (g + 1) * ARRIVE, pair_wait, 0)
        steps = []
        for i in range(ARRIVE):
            owner = chip_at(chip, g * ARRIVE + i, -1)
            steps += [2 * owner, 2 * owner + 1]
        for j in steps:
            block = mod_recv[j].astype(jnp.float32)
            mods[j, pl.ds(0, n_rows), :] = 0.5 * (1.0 + block[:n_rows])
            mods[j, pl.ds(n_rows, n_rows), :] = 0.5 * block[n_rows:2 * n_rows]
            mods[j, pl.ds(2 * n_rows, 1), :] = (block[2 * n_rows:2 * n_rows + 1] + block[2 * n_rows + 1:2 * n_rows + 2]) + block[2 * n_rows + 2:2 * n_rows + 3]
        acc = None
        for n in range(hidden // TILE):
            parts = []
            for j in steps:
                halves = []
                for c in range(n * (TILE // 128), (n + 1) * (TILE // 128)):
                    h = p0[:, c * 128:(c + 1) * 128] * mods[j, pl.ds(c, 1), :] + mods[j, pl.ds(n_rows + c, 1), :]
                    halves.append(half_gelu(h).astype(jnp.bfloat16))
                parts.append(jnp.concatenate(halves, axis=1))
            act = jnp.concatenate(parts, axis=0)
            prod = jnp.dot(act, w2[n * TILE:(n + 1) * TILE, :], preferred_element_type=jnp.float32)
            acc = prod if acc is None else acc + prod
        for i, j in enumerate(steps):
            drift[j] = mods[j, pl.ds(2 * n_rows, 1), :][:, :chans] * acc[i * CHUNKS * tok:(i + 1) * CHUNKS * tok, :]
        return carry

    lax.fori_loop(0, n_chips // ARRIVE, first_sweep, 0)

    def first_prefix(j, total):
        new = (x0[...] + total).astype(jnp.bfloat16)
        for q in range(CHUNKS):
            xbf[q, pl.ds(pl.multiple_of(j * tok, tok), tok), :] = new[q * tok:(q + 1) * tok]
        return total + drift[j]

    lax.fori_loop(0, n_time, first_prefix, jnp.zeros((CHUNKS * tok, chans), jnp.float32), unroll=8)

    steps = ROWS // tok

    def block_step(q, b, carry):
        acc = None
        x = xbf[q, pl.ds(pl.multiple_of(b * ROWS, ROWS), ROWS), :]
        for n in range(hidden // TILE):
            pre = jnp.dot(x, w1_ref[:, n * TILE:(n + 1) * TILE], preferred_element_type=jnp.float32)
            parts = []
            for s in range(steps):
                j = b * steps + s
                halves = []
                for half in range(TILE // 128):
                    c = n * (TILE // 128) + half
                    p = pre[s * tok:(s + 1) * tok, half * 128:(half + 1) * 128]
                    h = p * mods[j, pl.ds(c, 1), :] + mods[j, pl.ds(n_rows + c, 1), :]
                    halves.append(half_gelu(h).astype(jnp.bfloat16))
                parts.append(jnp.concatenate(halves, axis=1))
            act = jnp.concatenate(parts, axis=0)
            prod = jnp.dot(act, w2[n * TILE:(n + 1) * TILE, :], preferred_element_type=jnp.float32)
            acc = prod if acc is None else acc + prod
        start = x0[pl.ds(pl.multiple_of(q * tok, tok), tok), :]
        total = prefix[...]
        for s in range(steps):
            j = b * steps + s
            new = start + total
            xbf[q, pl.ds(pl.multiple_of(j * tok, tok), tok), :] = new.astype(jnp.bfloat16)
            send[q, j, :, 0:chans] = new[:GROUP]
            send[q, j, :, chans:2 * chans] = new[GROUP:]
            total = total + mods[j, pl.ds(2 * n_rows, 1), :][:, :chans] * acc[s * tok:(s + 1) * tok, :]
        prefix[...] = total
        return carry

    def chunk(q, carry):
        def sweep(i, carry):
            prefix[...] = jnp.zeros_like(prefix)
            return lax.fori_loop(0, n_time // steps, functools.partial(block_step, q), carry)

        lax.fori_loop(1, SWEEPS, sweep, 0)

        def out_copy(dst):
            return pltpu.make_async_remote_copy(
                src_ref=send.at[q, dst], dst_ref=recv.at[q, me], send_sem=out_send_sem, recv_sem=out_recv_sem.at[q],
                device_id={'time': dst}, device_id_type=MESH)

        def send_out(i, carry):
            other = chip_at(chip, n_chips - 1 - i, 1)
            out_copy(2 * other + core).start()
            out_copy(2 * other + 1 - core).start()
            return carry

        lax.fori_loop(0, n_chips - 1, send_out, 0)
        out_copy(partner).start()
        recv[q, me] = send[q, me]
        return carry

    lax.fori_loop(0, CHUNKS, chunk, 0)

    half_block = mod_recv.at[pl.ds(0, n_chips)]
    wait_bytes(half_block, pair_send_sem)
    wait_bytes(mod_recv.at[pl.ds(0, n_chips - 1)], mod_send_sem)
    for q in range(CHUNKS):
        wait_bytes(recv.at[q, pl.ds(0, n_time - 1)], out_recv_sem.at[q])
        for i in range(n_time * GROUP // 128):
            rows = recv[q, i * (128 // GROUP):(i + 1) * (128 // GROUP)].reshape(128, 2 * chans).T
            at = (q * n_time * GROUP) + i * 128
            out_ref[:, at:at + 128] = rows[:chans]
            out_ref[:, tokens // 2 + at:tokens // 2 + at + 128] = rows[chans:]
    wait_bytes(recv.at[:, pl.ds(0, n_time - 1)], out_send_sem)


def solution(mesh):
    n_time = mesh.shape['time']

    def per_device(x_init, w_in, w_out, mod_scale, mod_shift, step_size):
        _, tokens, chans = x_init.shape
        hidden = w_in.shape[1]
        tok = 2 * GROUP
        f32, bf16 = jnp.float32, jnp.bfloat16
        vmem = pl.BlockSpec(memory_space=pltpu.VMEM)
        out = pl.pallas_call(
            functools.partial(kernel, n_time),
            out_shape=jax.ShapeDtypeStruct((chans, tokens), f32),
            in_specs=[pl.BlockSpec(memory_space=pl.ANY), vmem, vmem, vmem, vmem, vmem],
            out_specs=vmem,
            scratch_shapes=[
                pltpu.VMEM((2 * CHUNKS, chans, 128), f32),
                pltpu.VMEM((2 * CHUNKS, 128, chans), f32),
                pltpu.VMEM((CHUNKS * tok, chans), f32),
                pltpu.VMEM((hidden, chans), bf16),
                pltpu.VMEM((32, 128), bf16),
                pltpu.VMEM((n_time, 32, 128), bf16),
                pltpu.VMEM((n_time, 32, 128), f32),
                pltpu.VMEM((CHUNKS * tok, hidden), f32),
                pltpu.VMEM((n_time, CHUNKS * tok, chans), f32),
                pltpu.VMEM((CHUNKS, n_time * tok, chans), bf16),
                pltpu.VMEM((CHUNKS, n_time, GROUP, 2 * chans), f32),
                pltpu.VMEM((CHUNKS, n_time, GROUP, 2 * chans), f32),
                pltpu.VMEM((tok, chans), f32),
                pltpu.SemaphoreType.DMA((2 * CHUNKS,)),
                pltpu.SemaphoreType.DMA,
                pltpu.SemaphoreType.DMA((n_time // 2,)),
                pltpu.SemaphoreType.DMA,
                pltpu.SemaphoreType.DMA((n_time // 2,)),
                pltpu.SemaphoreType.DMA,
                pltpu.SemaphoreType.DMA((CHUNKS,)),
            ],
            compiler_params=pltpu.CompilerParams(has_side_effects=True, collective_id=0),
            name='sweeps',
        )(x_init[0].T, w_in, w_out.T, mod_scale, mod_shift, step_size[None])
        return out.T.reshape(1, 1, tokens, chans)

    return jax.shard_map(per_device, mesh=mesh, in_specs=(P('data'), P(), P(), P('time'), P('time'), P('time')), out_specs=P('time', 'data'), check_vma=False)
```

time: 82.5 us -> 80.6 us (0.977)
  Pallas kernels: 81.6 us -> 77.4 us
  local copies, waits for them, and re-layouts: 0 us -> 2.27 us
    pallas_call x1 -> x0, Pallas kernels: 2.53 us -> none  [per_device(): pl.pallas_call(spread, out_shape=jax.ShapeDtypeStruct((chans, tokens), jn...]
    unnamed x0 -> x1, local copies, waits for them, and re-layouts: none -> 2.27 us
    pallas_call x1, Pallas kernels: 79.1 us -> 77.4 us  [per_device(): pl.pallas_call(functools.partial(kernel, n_time), out_shape=jax.ShapeDtyp...]
where the time goes in v2:
time: 80.6 us; the launch traced here: 80.4 us
  Pallas kernels  77.4 us (96%)
  local copies, waits for them, and re-layouts  2.27 us (3%)
    pallas_call x1, Pallas kernels, per_device(): pl.pallas_call(functools.partial(kernel, n_time), out_shape=jax.ShapeDtyp...  77.4 us
    unnamed x1, local copies, waits for them, and re-layouts  2.27 us

profile of v2, /device:TPU:1, one launch (start us, length us, event | category | flops | bytes accessed | tf_op | source)
XLA Modules:
  0.0 80.4 jit_solution(13527679295069417432)
XLA Ops:
  0.7 77.4 %sweeps.1 = f32[64,4096]{1,0:T(8,128)} custom-call(f32[64,4096]{1,0:T(8,128)} %bitcast.10, bf16[64,1536]{1,0:T(8,128)(2,1)} %w1_ref.1, bf16[64,1536]{1,0:T(8,128)(2,1)} %bitcast.11, bf16[1,1536]{1,0:T(2,128)(2,1)} %scale_ref.1, bf16[1,1536]{1,0:T(2,128)(2,1)} %shift_ref.1, f32[1,1]{1,0:T(1,128)} %bitcast.8.step_ref), custom_call_target="tpu_custom_call" | custom-call | tf_op jit(solution)/shard_map/sweeps/pallas_call | solution.py:243
  78.1 2.3 %copy.9 = f32[1,1,4096,64]{2,3,1,0:T(8,128)} copy(f32[1,1,4096,64]{2,3,1,0:T(8,128)} %bitcast.9) | data formatting | bytes 2097152

commit v3 on v2

--- a/solution.py
+++ b/solution.py
@@ -16,6 +16,7 @@
 GROUP = 8
 SIDE = 4
 ARRIVE = 8
+AHEAD = 4
 DEV_STRIDE = 45
 MESH = pl.DeviceIdType.MESH
 
@@ -41,9 +42,9 @@
     return out
 
 
-def kernel(n_time, x_hbm, w1_ref, w2t_ref, scale_ref, shift_ref, step_ref, out_ref,
-           xcol, xrow, x0, w2, mod_send, mod_recv, mods, p0, drift, xbf, send, recv, prefix,
-           x_sem, mod_send_sem, mod_recv_sem, pair_send_sem, pair_recv_sem, out_send_sem, out_recv_sem):
+def kernel(n_time, x_hbm, w1_hbm, w2t_hbm, scale_hbm, shift_hbm, step_ref, out_ref,
+           w1_ref, w2t_ref, scale_ref, shift_ref, xcol, xrow, x0, w2, mod_send, mod_recv, mods, p0, drift, xbf, send, recv, prefix,
+           load_sem, x_sem, mod_send_sem, mod_recv_sem, pair_send_sem, pair_recv_sem, out_send_sem, out_recv_sem):
     me = lax.axis_index('time')
     n_chips = n_time // 2
     chip = me // 2
@@ -62,6 +63,10 @@
 
     lax.fori_loop(1, n_time, arrive, 0)
 
+    loads = [pltpu.make_async_copy(src, dst, load_sem.at[i]) for i, (src, dst) in enumerate(
+        [(scale_hbm, scale_ref), (shift_hbm, shift_ref), (w2t_hbm, w2t_ref), (w1_hbm, w1_ref)])]
+    for load in loads:
+        load.start()
     x_copies = []
     for i in range(2 * CHUNKS):
         start = (i % 2) * (tokens // 2) + (i // 2) * (tokens // 2 // CHUNKS) + (me * GROUP // 128) * 128
@@ -69,6 +74,8 @@
             x_hbm.at[:, pl.ds(pl.multiple_of(start, 128), 128)], xcol.at[i], x_sem.at[i]))
         x_copies[-1].start()
 
+    loads[0].wait()
+    loads[1].wait()
     for c in range(n_rows):
         mod_send[pl.ds(c, 1), :] = scale_ref[:, c * 128:(c + 1) * 128]
         mod_send[pl.ds(n_rows + c, 1), :] = shift_ref[:, c * 128:(c + 1) * 128]
@@ -82,12 +89,14 @@
     mod_send[pl.ds(2 * n_rows + 2, 1), :] = low
     mod_recv[me] = mod_send[...]
 
+    loads[2].wait()
     w2[...] = w2t_ref[...].astype(jnp.float32).T.astype(jnp.bfloat16)
     lo = pl.ds(pl.multiple_of(lax.rem(me * GROUP, 128), GROUP), GROUP)
     for i in range(2 * CHUNKS):
         x_copies[i].wait()
         xrow[i] = xcol[i].T
         x0[i * GROUP:(i + 1) * GROUP, :] = xrow[i, lo, :]
+    loads[3].wait()
     x0_rounded = x0[...].astype(jnp.bfloat16)
     for n in range(hidden // TILE):
         p0[:, n * TILE:(n + 1) * TILE] = jnp.dot(
@@ -119,22 +128,34 @@
         pair_copy(k, me, mod_send).wait_recv()
         return carry
 
-    pair_copy(0, me, mod_send).start()
-    lax.fori_loop(1, n_chips, send_mod, 0)
-    lax.fori_loop(1, ARRIVE, relay, 0)
-
-    def first_sweep(g, carry):
-        lax.fori_loop((g + 1) * ARRIVE, jnp.minimum((g + 2) * ARRIVE, n_chips), relay, 0)
-        lax.fori_loop(g * ARRIVE, (g + 1) * ARRIVE, pair_wait, 0)
+    def group(g):
         steps = []
         for i in range(ARRIVE):
             owner = chip_at(chip, g * ARRIVE + i, -1)
             steps += [2 * owner, 2 * owner + 1]
-        for j in steps:
+        return steps
+
+    def unpack(g):
+        for j in group(g):
             block = mod_recv[j].astype(jnp.float32)
             mods[j, pl.ds(0, n_rows), :] = 0.5 * (1.0 + block[:n_rows])
             mods[j, pl.ds(n_rows, n_rows), :] = 0.5 * block[n_rows:2 * n_rows]
             mods[j, pl.ds(2 * n_rows, 1), :] = (block[2 * n_rows:2 * n_rows + 1] + block[2 * n_rows + 1:2 * n_rows + 2]) + block[2 * n_rows + 2:2 * n_rows + 3]
+
+    def each(g, body):
+        lax.fori_loop(jnp.minimum(g * ARRIVE, n_chips), jnp.minimum((g + 1) * ARRIVE, n_chips), body, 0)
+
+    pair_copy(0, me, mod_send).start()
+    lax.fori_loop(1, AHEAD * ARRIVE, send_mod, 0)
+    lax.fori_loop(1, 2 * ARRIVE, relay, 0)
+    each(0, pair_wait)
+    unpack(0)
+
+    def first_sweep(g, carry):
+        each(g + AHEAD, send_mod)
+        each(g + 2, relay)
+        each(g + 1, pair_wait)
+        steps = group(g)
         acc = None
         for n in range(hidden // TILE):
             parts = []
@@ -149,6 +170,7 @@
             acc = prod if acc is None else acc + prod
         for i, j in enumerate(steps):
             drift[j] = mods[j, pl.ds(2 * n_rows, 1), :][:, :chans] * acc[i * CHUNKS * tok:(i + 1) * CHUNKS * tok, :]
+        unpack(lax.rem(g + 1, n_chips // ARRIVE))
         return carry
 
     lax.fori_loop(0, n_chips // ARRIVE, first_sweep, 0)
@@ -243,9 +265,13 @@
         out = pl.pallas_call(
             functools.partial(kernel, n_time),
             out_shape=jax.ShapeDtypeStruct((chans, tokens), f32),
-            in_specs=[pl.BlockSpec(memory_space=pl.ANY), vmem, vmem, vmem, vmem, vmem],
+            in_specs=[pl.BlockSpec(memory_space=pltpu.HBM)] * 5 + [vmem],
             out_specs=vmem,
             scratch_shapes=[
+                pltpu.VMEM((chans, hidden), bf16),
+                pltpu.VMEM((chans, hidden), bf16),
+                pltpu.VMEM((1, hidden), bf16),
+                pltpu.VMEM((1, hidden), bf16),
                 pltpu.VMEM((2 * CHUNKS, chans, 128), f32),
                 pltpu.VMEM((2 * CHUNKS, 128, chans), f32),
                 pltpu.VMEM((CHUNKS * tok, chans), f32),
@@ -259,6 +285,7 @@
                 pltpu.VMEM((CHUNKS, n_time, GROUP, 2 * chans), f32),
                 pltpu.VMEM((CHUNKS, n_time, GROUP, 2 * chans), f32),
                 pltpu.VMEM((tok, chans), f32),
+                pltpu.SemaphoreType.DMA((4,)),
                 pltpu.SemaphoreType.DMA((2 * CHUNKS,)),
                 pltpu.SemaphoreType.DMA,
                 pltpu.SemaphoreType.DMA((n_time // 2,)),
@@ -267,7 +294,7 @@
                 pltpu.SemaphoreType.DMA,
                 pltpu.SemaphoreType.DMA((CHUNKS,)),
             ],
-            compiler_params=pltpu.CompilerParams(has_side_effects=True, collective_id=0),
+            compiler_params=pltpu.CompilerParams(has_side_effects=True, collective_id=0, vmem_limit_bytes=32 * 1024 * 1024),
             name='sweeps',
         )(x_init[0].T, w_in, w_out.T, mod_scale, mod_shift, step_size[None])
         return out.T.reshape(1, 1, tokens, chans)

time: 80.6 us -> 83.9 us (1.041)
  local copies, waits for them, and re-layouts: 2.27 us -> 4.77 us
    unnamed x1 -> x11, local copies, waits for them, and re-layouts: 2.27 us -> 4.77 us
where the time goes in v3:
time: 83.9 us; the launch traced here: 83.6 us
  Pallas kernels  78.2 us (93%)
  local copies, waits for them, and re-layouts  4.77 us (6%)
    pallas_call x1, Pallas kernels, per_device(): pl.pallas_call(functools.partial(kernel, n_time), out_shape=jax.ShapeDtyp...  78.2 us
    unnamed x11, local copies, waits for them, and re-layouts  4.77 us

profile of v3, /device:TPU:1, one launch (start us, length us, event | category | flops | bytes accessed | tf_op | source)
XLA Modules:
  0.0 83.6 jit_solution(8580126122235870672)
XLA Ops:
  0.0 0.0 copy-start.3
  0.7 0.0 copy-done.3
  0.7 0.0 copy-start
  0.7 1.2 %copy-done = f32[1,4096,64]{1,2,0:T(8,128)S(1)} copy-done((f32[1,4096,64]{1,2,0:T(8,128)S(1)}, f32[1,4096,64]{1,2,0:T(8,128)}, u32[]{:S(2)}) %copy-start) | copy-done | bytes 1048600
  1.9 0.0 copy-start.1
  1.9 0.9 %copy-done.1 = bf16[64,1536]{1,0:T(8,128)(2,1)S(1)} copy-done((bf16[64,1536]{1,0:T(8,128)(2,1)S(1)}, bf16[64,1536]{1,0:T(8,128)(2,1)}, u32[]{:S(2)}) %copy-start.1) | copy-done | bytes 196632
  2.8 0.0 copy-start.2
  2.8 0.9 %copy-done.2 = bf16[1536,64]{0,1:T(8,128)(2,1)S(1)} copy-done((bf16[1536,64]{0,1:T(8,128)(2,1)S(1)}, bf16[1536,64]{0,1:T(8,128)(2,1)}, u32[]{:S(2)}) %copy-start.2) | copy-done | bytes 196632
  3.8 0.0 copy-start.4
  3.8 0.7 copy-done.4
  4.5 78.2 %sweeps.1 = f32[64,4096]{1,0:T(8,128)S(1)} custom-call(f32[64,4096]{1,0:T(8,128)S(1)} %bitcast.10, bf16[64,1536]{1,0:T(8,128)(2,1)S(1)} %copy-done.1, bf16[64,1536]{1,0:T(8,128)(2,1)S(1)} %bitcast.11, bf16[1,1536]{1,0:T(2,128)(2,1)S(1)} %copy-done.3, bf16[1,1536]{1,0:T(2,128)(2,1)S(1)} %copy-done.4, f32[1,1]{1,0:T(1,128)} %bitcast.8.step_ref), custom_call_target="tpu_custom_call" | custom-call | tf_op jit(solution)/shard_map/sweeps/pallas_call | solution.py:265
  82.7 1.0 %copy.9 = f32[1,1,4096,64]{2,3,1,0:T(8,128)} copy(f32[1,1,4096,64]{2,3,1,0:T(8,128)S(1)} %bitcast.9) | data formatting | bytes 2097152
Async XLA Ops:
  0.0 0.7 copy-start.3
  0.7 1.2 %copy-start = (f32[1,4096,64]{1,2,0:T(8,128)S(1)}, f32[1,4096,64]{1,2,0:T(8,128)}, u32[]{:S(2)}) copy-start(f32[1,4096,64]{1,2,0:T(8,128)} %param.6) | copy-start | bytes 3145732
  1.9 0.9 %copy-start.1 = (bf16[64,1536]{1,0:T(8,128)(2,1)S(1)}, bf16[64,1536]{1,0:T(8,128)(2,1)}, u32[]{:S(2)}) copy-start(bf16[64,1536]{1,0:T(8,128)(2,1)} %w1_hbm.1) | copy-start | bytes 589828
  2.8 0.9 %copy-start.2 = (bf16[1536,64]{0,1:T(8,128)(2,1)S(1)}, bf16[1536,64]{0,1:T(8,128)(2,1)}, u32[]{:S(2)}) copy-start(bf16[1536,64]{0,1:T(8,128)(2,1)} %param.8) | copy-start | bytes 589828
  3.8 0.7 copy-start.4

commit v4 on v3

--- a/solution.py
+++ b/solution.py
@@ -30,16 +30,11 @@
     pltpu.make_async_copy(ref, ref, sem).wait()
 
 
+NEAR = (0, 1, 3, 2)
+
+
 def hop(t):
     return t + (t // 2) * (1 - 2 * lax.rem(t, 2))
-
-
-def chip_at(chip, k, sign):
-    pos, out, scale = chip, 0, 1
-    for _ in range(3):
-        out = out + scale * lax.rem(lax.rem(pos, SIDE) + sign * hop(lax.rem(k, SIDE)) + SIDE, SIDE)
-        pos, k, scale = pos // SIDE, k // SIDE, scale * SIDE
-    return out
 
 
 def kernel(n_time, x_hbm, w1_hbm, w2t_hbm, scale_hbm, shift_hbm, step_ref, out_ref,
@@ -104,58 +99,66 @@
 
     pl.semaphore_wait(barrier, n_time - 1)
 
-    def mod_copy(k):
+    place_x, place_y, place_z = lax.rem(chip, SIDE), lax.rem(chip // SIDE, SIDE), chip // (SIDE * SIDE)
+
+    def along(place, step):
+        return lax.rem(place + step + SIDE, SIDE)
+
+    def group(g, sign):
+        z = along(place_z, sign * hop(g // 2)) * (SIDE * SIDE)
+        chips = []
+        for i in range(2):
+            zy = z + along(place_y, sign * hop(2 * lax.rem(g, 2) + i)) * SIDE
+            chips += [zy + along(place_x, sign * step) for step in NEAR]
+        return chips
+
+    def mod_copy(k, dst):
         return pltpu.make_async_remote_copy(
             src_ref=mod_send, dst_ref=mod_recv.at[me], send_sem=mod_send_sem, recv_sem=mod_recv_sem.at[k],
-            device_id={'time': chip_at(chip, k, 1) * 2 + core}, device_id_type=MESH)
+            device_id={'time': dst}, device_id_type=MESH)
 
     def pair_copy(k, src, src_ref):
         return pltpu.make_async_remote_copy(
             src_ref=src_ref, dst_ref=mod_recv.at[src], send_sem=pair_send_sem, recv_sem=pair_recv_sem.at[k],
             device_id={'time': partner}, device_id_type=MESH)
 
-    def send_mod(k, carry):
-        mod_copy(k).start()
-        return carry
-
-    def relay(k, carry):
-        mod_copy(k).wait_recv()
-        src = chip_at(chip, k, -1) * 2 + core
-        pair_copy(k, src, mod_recv.at[src]).start()
-        return carry
-
-    def pair_wait(k, carry):
-        pair_copy(k, me, mod_send).wait_recv()
-        return carry
-
-    def group(g):
-        steps = []
+    def send_group(g, first=0):
+        for i, other in enumerate(group(g, 1)[first:], first):
+            mod_copy(g * ARRIVE + i, 2 * other + core).start()
+
+    def relay_group(g, first=0):
+        for i, other in enumerate(group(g, -1)[first:], first):
+            mod_copy(g * ARRIVE + i, me).wait_recv()
+            src = 2 * other + core
+            pair_copy(g * ARRIVE + i, src, mod_recv.at[src]).start()
+
+    def pair_wait(g):
         for i in range(ARRIVE):
-            owner = chip_at(chip, g * ARRIVE + i, -1)
-            steps += [2 * owner, 2 * owner + 1]
-        return steps
+            pair_copy(g * ARRIVE + i, me, mod_send).wait_recv()
 
     def unpack(g):
-        for j in group(g):
-            block = mod_recv[j].astype(jnp.float32)
-            mods[j, pl.ds(0, n_rows), :] = 0.5 * (1.0 + block[:n_rows])
-            mods[j, pl.ds(n_rows, n_rows), :] = 0.5 * block[n_rows:2 * n_rows]
-            mods[j, pl.ds(2 * n_rows, 1), :] = (block[2 * n_rows:2 * n_rows + 1] + block[2 * n_rows + 1:2 * n_rows + 2]) + block[2 * n_rows + 2:2 * n_rows + 3]
-
-    def each(g, body):
-        lax.fori_loop(jnp.minimum(g * ARRIVE, n_chips), jnp.minimum((g + 1) * ARRIVE, n_chips), body, 0)
-
+        for other in group(g, -1):
+            for j in (2 * other, 2 * other + 1):
+                block = mod_recv[j].astype(jnp.float32)
+                mods[j, pl.ds(0, n_rows), :] = 0.5 * (1.0 + block[:n_rows])
+                mods[j, pl.ds(n_rows, n_rows), :] = 0.5 * block[n_rows:2 * n_rows]
+                mods[j, pl.ds(2 * n_rows, 1), :] = (block[2 * n_rows:2 * n_rows + 1] + block[2 * n_rows + 1:2 * n_rows + 2]) + block[2 * n_rows + 2:2 * n_rows + 3]
+
+    n_groups = n_chips // ARRIVE
     pair_copy(0, me, mod_send).start()
-    lax.fori_loop(1, AHEAD * ARRIVE, send_mod, 0)
-    lax.fori_loop(1, 2 * ARRIVE, relay, 0)
-    each(0, pair_wait)
+    send_group(0, 1)
+    for g in range(1, AHEAD):
+        send_group(g)
+    relay_group(0, 1)
+    relay_group(1)
+    pair_wait(0)
     unpack(0)
 
     def first_sweep(g, carry):
-        each(g + AHEAD, send_mod)
-        each(g + 2, relay)
-        each(g + 1, pair_wait)
-        steps = group(g)
+        pl.when(g + AHEAD < n_groups)(lambda: send_group(g + AHEAD))
+        pl.when(g + 2 < n_groups)(lambda: relay_group(g + 2))
+        pl.when(g + 1 < n_groups)(lambda: pair_wait(g + 1))
+        steps = [2 * other + c for other in group(g, -1) for c in range(2)]
         acc = None
         for n in range(hidden // TILE):
             parts = []
@@ -170,10 +173,10 @@
             acc = prod if acc is None else acc + prod
         for i, j in enumerate(steps):
             drift[j] = mods[j, pl.ds(2 * n_rows, 1), :][:, :chans] * acc[i * CHUNKS * tok:(i + 1) * CHUNKS * tok, :]
-        unpack(lax.rem(g + 1, n_chips // ARRIVE))
+        unpack(lax.rem(g + 1, n_groups))
         return carry
 
-    lax.fori_loop(0, n_chips // ARRIVE, first_sweep, 0)
+    lax.fori_loop(0, n_groups, first_sweep, 0)
 
     def first_prefix(j, total):
         new = (x0[...] + total).astype(jnp.bfloat16)
@@ -227,13 +230,10 @@
                 src_ref=send.at[q, dst], dst_ref=recv.at[q, me], send_sem=out_send_sem, recv_sem=out_recv_sem.at[q],
                 device_id={'time': dst}, device_id_type=MESH)
 
-        def send_out(i, carry):
-            other = chip_at(chip, n_chips - 1 - i, 1)
+        for k in range(n_chips - 1, 0, -1):
+            other = (along(place_z, NEAR[k // (SIDE * SIDE)]) * SIDE + along(place_y, NEAR[k // SIDE % SIDE])) * SIDE + along(place_x, NEAR[k % SIDE])
             out_copy(2 * other + core).start()
             out_copy(2 * other + 1 - core).start()
-            return carry
-
-        lax.fori_loop(0, n_chips - 1, send_out, 0)
         out_copy(partner).start()
         recv[q, me] = send[q, me]
         return carry
@@ -294,7 +294,7 @@
                 pltpu.SemaphoreType.DMA,
                 pltpu.SemaphoreType.DMA((CHUNKS,)),
             ],
-            compiler_params=pltpu.CompilerParams(has_side_effects=True, collective_id=0, vmem_limit_bytes=32 * 1024 * 1024),
+            compiler_params=pltpu.CompilerParams(has_side_effects=True, collective_id=0),
             name='sweeps',
         )(x_init[0].T, w_in, w_out.T, mod_scale, mod_shift, step_size[None])
         return out.T.reshape(1, 1, tokens, chans)

time: 83.9 us -> 79.1 us (0.943)
  local copies, waits for them, and re-layouts: 4.77 us -> 2.27 us
  Pallas kernels: 78.2 us -> 76 us
    unnamed x11 -> x1, local copies, waits for them, and re-layouts: 4.77 us -> 2.27 us
    pallas_call x1, Pallas kernels: 78.2 us -> 76 us  [per_device(): pl.pallas_call(functools.partial(kernel, n_time), out_shape=jax.ShapeDtyp...]
where the time goes in v4:
time: 79.1 us; the launch traced here: 79 us
  Pallas kernels  76 us (96%)
  local copies, waits for them, and re-layouts  2.27 us (3%)
    pallas_call x1, Pallas kernels, per_device(): pl.pallas_call(functools.partial(kernel, n_time), out_shape=jax.ShapeDtyp...  76 us
    unnamed x1, local copies, waits for them, and re-layouts  2.27 us

profile of v4, /device:TPU:1, one launch (start us, length us, event | category | flops | bytes accessed | tf_op | source)
XLA Modules:
  0.0 79.0 jit_solution(15480801206360802548)
XLA Ops:
  0.7 76.0 %sweeps.1 = f32[64,4096]{1,0:T(8,128)} custom-call(f32[64,4096]{1,0:T(8,128)} %bitcast.10, bf16[64,1536]{1,0:T(8,128)(2,1)} %w1_hbm.1, bf16[64,1536]{1,0:T(8,128)(2,1)} %bitcast.11, bf16[1,1536]{1,0:T(2,128)(2,1)} %scale_hbm.1, bf16[1,1536]{1,0:T(2,128)(2,1)} %shift_hbm.1, f32[1,1]{1,0:T(1,128)} %bitcast.8.step_ref), custom_call_target="tpu_custom_call" | custom-call | tf_op jit(solution)/shard_map/sweeps/pallas_call | solution.py:265
  76.7 2.3 %copy.9 = f32[1,1,4096,64]{2,3,1,0:T(8,128)} copy(f32[1,1,4096,64]{2,3,1,0:T(8,128)} %bitcast.9) | data formatting | bytes 2097152

commit v5 on v4

--- a/solution.py
+++ b/solution.py
@@ -14,9 +14,9 @@
 ROWS = 1024
 CHUNKS = 2
 GROUP = 8
+SPREAD = 4
 SIDE = 4
 ARRIVE = 8
-AHEAD = 4
 DEV_STRIDE = 45
 MESH = pl.DeviceIdType.MESH
 
@@ -38,8 +38,8 @@
 
 
 def kernel(n_time, x_hbm, w1_hbm, w2t_hbm, scale_hbm, shift_hbm, step_ref, out_ref,
-           w1_ref, w2t_ref, scale_ref, shift_ref, xcol, xrow, x0, w2, mod_send, mod_recv, mods, p0, drift, xbf, send, recv, prefix,
-           load_sem, x_sem, mod_send_sem, mod_recv_sem, pair_send_sem, pair_recv_sem, out_send_sem, out_recv_sem):
+           w1_ref, w2t_ref, scale_ref, shift_ref, xcol, xrow, x0, w2, mod_send, mod_recv, mods, p0, drift, xbf, send, prefix,
+           load_sem, x_sem, mod_send_sem, mod_recv_sem, pair_send_sem, pair_recv_sem, out_send_sem, out_recv_sem, own_sem):
     me = lax.axis_index('time')
     n_chips = n_time // 2
     chip = me // 2
@@ -147,7 +147,7 @@
     n_groups = n_chips // ARRIVE
     pair_copy(0, me, mod_send).start()
     send_group(0, 1)
-    for g in range(1, AHEAD):
+    for g in range(1, n_groups):
         send_group(g)
     relay_group(0, 1)
     relay_group(1)
@@ -155,7 +155,6 @@
     unpack(0)
 
     def first_sweep(g, carry):
-        pl.when(g + AHEAD < n_groups)(lambda: send_group(g + AHEAD))
         pl.when(g + 2 < n_groups)(lambda: relay_group(g + 2))
         pl.when(g + 1 < n_groups)(lambda: pair_wait(g + 1))
         steps = [2 * other + c for other in group(g, -1) for c in range(2)]
@@ -218,6 +217,9 @@
         prefix[...] = total
         return carry
 
+    def own_copy(q):
+        return pltpu.make_async_copy(send.at[q, me], out_ref.at[q, me], own_sem.at[q])
+
     def chunk(q, carry):
         def sweep(i, carry):
             prefix[...] = jnp.zeros_like(prefix)
@@ -227,7 +229,7 @@
 
         def out_copy(dst):
             return pltpu.make_async_remote_copy(
-                src_ref=send.at[q, dst], dst_ref=recv.at[q, me], send_sem=out_send_sem, recv_sem=out_recv_sem.at[q],
+                src_ref=send.at[q, dst], dst_ref=out_ref.at[q, me], send_sem=out_send_sem, recv_sem=out_recv_sem.at[q],
                 device_id={'time': dst}, device_id_type=MESH)
 
         for k in range(n_chips - 1, 0, -1):
@@ -235,7 +237,7 @@
             out_copy(2 * other + core).start()
             out_copy(2 * other + 1 - core).start()
         out_copy(partner).start()
-        recv[q, me] = send[q, me]
+        own_copy(q).start()
         return carry
 
     lax.fori_loop(0, CHUNKS, chunk, 0)
@@ -244,13 +246,31 @@
     wait_bytes(half_block, pair_send_sem)
     wait_bytes(mod_recv.at[pl.ds(0, n_chips - 1)], mod_send_sem)
     for q in range(CHUNKS):
-        wait_bytes(recv.at[q, pl.ds(0, n_time - 1)], out_recv_sem.at[q])
-        for i in range(n_time * GROUP // 128):
-            rows = recv[q, i * (128 // GROUP):(i + 1) * (128 // GROUP)].reshape(128, 2 * chans).T
-            at = (q * n_time * GROUP) + i * 128
-            out_ref[:, at:at + 128] = rows[:chans]
-            out_ref[:, tokens // 2 + at:tokens // 2 + at + 128] = rows[chans:]
-    wait_bytes(recv.at[:, pl.ds(0, n_time - 1)], out_send_sem)
+        own_copy(q).wait()
+        wait_bytes(out_ref.at[q, pl.ds(0, n_time - 1)], out_recv_sem.at[q])
+    wait_bytes(send.at[:, pl.ds(0, n_time - 1)], out_send_sem)
+
+
+def spread(rows_hbm, out_hbm, rows, cols, in_sem, out_sem):
+    chans, tokens = out_hbm.shape
+    part = rows_hbm.shape[0] // SPREAD
+    loads = [pltpu.make_async_copy(rows_hbm.at[pl.ds(i * part, part)], rows.at[pl.ds(i * part, part)], in_sem.at[i])
+             for i in range(SPREAD)]
+    for load in loads:
+        load.start()
+    stores = []
+    for i in range(SPREAD):
+        loads[i].wait()
+        for at in range(i * part, (i + 1) * part, 128):
+            block = rows[at:at + 128, :].T
+            cols[:, at:at + 128] = block[:chans]
+            cols[:, tokens // 2 + at:tokens // 2 + at + 128] = block[chans:]
+        for half in range(2):
+            at = pl.ds(half * (tokens // 2) + i * part, part)
+            stores.append(pltpu.make_async_copy(cols.at[:, at], out_hbm.at[:, at], out_sem.at[2 * i + half]))
+            stores[-1].start()
+    for store in stores:
+        store.wait()
 
 
 def solution(mesh):
@@ -261,12 +281,12 @@
         hidden = w_in.shape[1]
         tok = 2 * GROUP
         f32, bf16 = jnp.float32, jnp.bfloat16
-        vmem = pl.BlockSpec(memory_space=pltpu.VMEM)
+        vmem, hbm = pl.BlockSpec(memory_space=pltpu.VMEM), pl.BlockSpec(memory_space=pltpu.HBM)
         out = pl.pallas_call(
             functools.partial(kernel, n_time),
-            out_shape=jax.ShapeDtypeStruct((chans, tokens), f32),
-            in_specs=[pl.BlockSpec(memory_space=pltpu.HBM)] * 5 + [vmem],
-            out_specs=vmem,
+            out_shape=jax.ShapeDtypeStruct((CHUNKS, n_time, GROUP, 2 * chans), f32),
+            in_specs=[hbm] * 5 + [vmem],
+            out_specs=hbm,
             scratch_shapes=[
                 pltpu.VMEM((chans, hidden), bf16),
                 pltpu.VMEM((chans, hidden), bf16),
@@ -283,7 +303,6 @@
                 pltpu.VMEM((n_time, CHUNKS * tok, chans), f32),
                 pltpu.VMEM((CHUNKS, n_time * tok, chans), bf16),
                 pltpu.VMEM((CHUNKS, n_time, GROUP, 2 * chans), f32),
-                pltpu.VMEM((CHUNKS, n_time, GROUP, 2 * chans), f32),
                 pltpu.VMEM((tok, chans), f32),
                 pltpu.SemaphoreType.DMA((4,)),
                 pltpu.SemaphoreType.DMA((2 * CHUNKS,)),
@@ -293,10 +312,21 @@
                 pltpu.SemaphoreType.DMA((n_time // 2,)),
                 pltpu.SemaphoreType.DMA,
                 pltpu.SemaphoreType.DMA((CHUNKS,)),
+                pltpu.SemaphoreType.DMA((CHUNKS,)),
             ],
             compiler_params=pltpu.CompilerParams(has_side_effects=True, collective_id=0),
             name='sweeps',
         )(x_init[0].T, w_in, w_out.T, mod_scale, mod_shift, step_size[None])
+        out = pl.pallas_call(
+            spread, out_shape=jax.ShapeDtypeStruct((chans, tokens), f32), in_specs=[hbm], out_specs=hbm,
+            scratch_shapes=[
+                pltpu.VMEM((tokens // 2, 2 * chans), f32),
+                pltpu.VMEM((chans, tokens), f32),
+                pltpu.SemaphoreType.DMA((SPREAD,)),
+                pltpu.SemaphoreType.DMA((2 * SPREAD,)),
+            ],
+            name='spread',
+        )(out.reshape(tokens // 2, 2 * chans))
         return out.T.reshape(1, 1, tokens, chans)
 
     return jax.shard_map(per_device, mesh=mesh, in_specs=(P('data'), P(), P(), P('time'), P('time'), P('time')), out_specs=P('time', 'data'), check_vma=False)

time: 79.1 us -> 73.5 us (0.929)
  Pallas kernels: 76 us -> 72.7 us
  local copies, waits for them, and re-layouts: 2.27 us -> 0 us
    pallas_call x1, Pallas kernels: 76 us -> 70.4 us  [per_device(): pl.pallas_call(functools.partial(kernel, n_time), out_shape=jax.ShapeDtyp...]
    pallas_call x0 -> x1, Pallas kernels: none -> 2.3 us  [per_device(): pl.pallas_call(spread, out_shape=jax.ShapeDtypeStruct((chans, tokens), f3...]
    unnamed x1 -> x0, local copies, waits for them, and re-layouts: 2.27 us -> none
where the time goes in v5:
time: 73.5 us; the launch traced here: 73.4 us
  Pallas kernels  72.7 us (99%)
    pallas_call x1, Pallas kernels, per_device(): pl.pallas_call(functools.partial(kernel, n_time), out_shape=jax.ShapeDtyp...  70.4 us
    pallas_call x1, Pallas kernels, per_device(): pl.pallas_call(spread, out_shape=jax.ShapeDtypeStruct((chans, tokens), f3...  2.3 us

profile of v5, /device:TPU:1, one launch (start us, length us, event | category | flops | bytes accessed | tf_op | source)
XLA Modules:
  0.0 73.4 jit_solution(8108486562582456151)
XLA Ops:
  0.7 70.4 %sweeps.1 = f32[2,128,8,128]{3,2,1,0:T(8,128)} custom-call(f32[64,4096]{1,0:T(8,128)} %bitcast.11, bf16[64,1536]{1,0:T(8,128)(2,1)} %w1_hbm.1, bf16[64,1536]{1,0:T(8,128)(2,1)} %bitcast.12, bf16[1,1536]{1,0:T(2,128)(2,1)} %scale_hbm.1, bf16[1,1536]{1,0:T(2,128)(2,1)} %shift_hbm.1, f32[1,1]{1,0:T(1,128)} %bitcast.9.step_ref), custom_call_target="tpu_custom_call" | custom-call | tf_op jit(solution)/shard_map/sweeps/pallas_call | solution.py:285
  71.1 2.3 %spread.1 = f32[64,4096]{1,0:T(8,128)} custom-call(f32[2048,128]{1,0:T(8,128)} %bitcast.10), custom_call_target="tpu_custom_call" | custom-call | tf_op jit(solution)/shard_map/spread/pallas_call | solution.py:320
